TPU v7x, 32 devices: a whole 2x2x4 slice. The times are simulated.
32 devices in a mesh: ctx: 16 (over z, y, core), head: 2 (over x).
Axes of the slice: x: 2, y: 2, z: 4, core: 2. Of those that a mesh axis runs over, the one named last changes fastest.
Arguments:
- queries: bfloat16 [2048, 2048], P('ctx', 'head'), may hold values from -100 to 100
- keys: bfloat16 [2048, 2048], P('ctx', 'head'), may hold values from -50 to 50
- values: bfloat16 [2048, 2048], P('ctx', 'head'), may hold values from -6 to 6
- out_weight: bfloat16 [2048, 4096], P('head'), may hold values from -0.125 to 0.125
- mixed_grad: bfloat16 [2048, 4096], P('ctx', 'head'), may hold values from -6 to 6
- lengths: int32 [16], replicated, may hold values from 1 to 384, 2048 in all
- dilation: int32 [16], P('head'), may hold values from 1 to 8
Outputs:
- mixed: bfloat16 [2048, 4096], P('ctx', 'head')
- grad_queries: bfloat16 [2048, 2048], P('ctx', 'head')
- grad_keys: bfloat16 [2048, 2048], P('ctx', 'head')
- grad_values: bfloat16 [2048, 2048], P('ctx', 'head')
Inputs may be any that keep to these rules, and one draw needn't show every extreme that they name: The lengths sum to 2048, and the longest document has exactly 384 tokens.
All inputs are finite; a program needn't handle non-finite values.
Results may differ from a plain program's by a relative error of at most 0.029.
Values may be sent and summed in bfloat16 or wider, within the bound.
A program may use at most 64 MiB of HBM per device.

v0:
```python
import functools
import jax
import jax.numpy as jnp
from jax import lax
from jax.experimental import pallas as pl
from jax.experimental.pallas import tpu as pltpu
from jax.sharding import PartitionSpec as P

HALF = 32
MAXD = 8
FAR = 1e6
NEG = -1e30


def attend_kernel(
    row_count, total, factor, first, index_ref, length_ref, dilation_ref,
    q_ref, go_ref, own_ref, a_ref, b_ref, po_ref, pa_ref,
    att_ref, gq_ref, own_t, a_t, b_t, po_t, pa_t, dist,
):
    slabs = (own_ref, a_ref, b_ref, po_ref, pa_ref)
    outs = (own_t, a_t, b_t, po_t, pa_t)

    @pl.when(pl.program_id(0) == 0)
    def _():
        me = index_ref[0]
        sign = 1 - 2 * lax.rem(me, 2)
        ends = [length_ref[0]]
        for n in range(1, length_ref.shape[0]):
            ends.append(ends[-1] + length_ref[n])

        def segment(pos):
            seg = jnp.zeros(pos.shape, jnp.int32)
            for end in ends:
                seg = seg + (pos >= end).astype(jnp.int32)
            return seg

        qpos = me * row_count + lax.broadcasted_iota(jnp.int32, (1, row_count), 1)
        qseg = segment(qpos)
        for i, off in enumerate((0, 2, -2, 1, -1)):
            kpos = (me + sign * off) * row_count + lax.broadcasted_iota(
                jnp.int32, (row_count, row_count), 0
            )
            same = (segment(kpos) == qseg) & (kpos >= 0) & (kpos < total)
            gap = jnp.abs(kpos - qpos).astype(jnp.float32)
            dist[pl.ds(i * row_count, row_count), :] = jnp.where(same, gap, FAR)

    spacing = jnp.full((1, row_count), dilation_ref[first + pl.program_id(0)], jnp.int32)
    inv = 1.0 / spacing.astype(jnp.float32)
    steps = dist[...] * inv
    whole = jnp.floor(steps + 0.5)
    mask = (whole <= HALF) & (jnp.abs(steps - whole) < 0.01)
    q = q_ref[...]
    go = go_ref[...]
    k = jnp.concatenate([r[0] for r in slabs], axis=0)
    v = jnp.concatenate([r[1] for r in slabs], axis=0)
    nt = (((1,), (1,)), ((), ()))
    tn = (((0,), (0,)), ((), ()))
    f32 = jnp.float32
    scores = lax.dot_general(k, q, nt, preferred_element_type=f32) * factor
    scores = jnp.where(mask, scores, NEG)
    top = jnp.max(scores, axis=0, keepdims=True)
    e = jnp.exp(scores - top)
    w = e * (1.0 / jnp.sum(e, axis=0, keepdims=True))
    p = w.astype(jnp.bfloat16)
    gp = lax.dot_general(v, go, nt, preferred_element_type=f32)
    delta = jnp.sum(w * gp, axis=0, keepdims=True)
    s = (w * (gp - delta)).astype(jnp.bfloat16)
    att_ref[...] = lax.dot_general(p, v, tn, preferred_element_type=f32).astype(jnp.bfloat16)
    gq_ref[...] = (
        lax.dot_general(s, k, tn, preferred_element_type=f32) * factor
    ).astype(jnp.bfloat16)
    kt = (jnp.dot(s, q, preferred_element_type=f32) * factor).astype(jnp.bfloat16)
    vt = jnp.dot(p, go, preferred_element_type=f32).astype(jnp.bfloat16)
    for i, out in enumerate(outs):
        out[0] = kt[i * row_count : (i + 1) * row_count]
        out[1] = vt[i * row_count : (i + 1) * row_count]


def attend(index, lengths, dilation, q, go, slabs, first, total, factor, width):
    rows, cols = q.shape[0], slabs[0].shape[2]
    heads = cols // width
    smem = pl.BlockSpec(memory_space=pltpu.SMEM)
    shared = pl.BlockSpec((rows, width), lambda h: (0, first + h))
    flat = pl.BlockSpec((rows, width), lambda h: (0, h))
    pair = pl.BlockSpec((2, rows, width), lambda h: (0, 0, h))
    one = jax.ShapeDtypeStruct((rows, cols), jnp.bfloat16)
    two = jax.ShapeDtypeStruct((2, rows, cols), jnp.bfloat16)
    return pl.pallas_call(
        functools.partial(attend_kernel, rows, total, factor, first),
        grid=(heads,),
        in_specs=[smem, smem, smem, shared, shared] + [pair] * 5,
        out_specs=[flat, flat] + [pair] * 5,
        out_shape=[one, one] + [two] * 5,
        scratch_shapes=[pltpu.VMEM((5 * rows, rows), jnp.float32)],
        compiler_params=pltpu.CompilerParams(dimension_semantics=("arbitrary",)),
        cost_estimate=pl.CostEstimate(
            flops=heads * 6 * 2 * 5 * rows * rows * width * 8,
            bytes_accessed=24 * 2 * rows * cols,
            transcendentals=heads * 5 * rows * rows,
        ),
    )(index, lengths, dilation, q, go, *slabs)


def per_device(queries, keys, values, out_weight, mixed_grad, lengths, dilation):
    rows = queries.shape[0]
    local_heads = dilation.shape[0]
    width = queries.shape[1] // local_heads
    factor = width ** (-0.5)
    count = lax.axis_size("ctx")
    sides = lax.axis_size("head")
    total = rows * count
    assert 2 * rows >= HALF * MAXD and count % 2 == 0
    index = lax.axis_index("ctx").astype(jnp.int32).reshape(1)

    inward = [
        (j, t) for j in range(count) for t in [j - 2 if j % 2 == 0 else j + 2] if 0 <= t < count
    ]
    outward = [(t, j) for j, t in inward]
    swapped = [(j, j ^ 1) for j in range(count)]

    def move(x, pairs):
        return lax.ppermute(x, "ctx", pairs)

    groups = 1
    gh = local_heads // groups
    cut = [slice(g * gh * width, (g + 1) * gh * width) for g in range(groups)]
    half = mixed_grad.shape[1]
    if sides == 2:
        other = lax.ppermute(mixed_grad, "head", [(0, 1), (1, 0)])
        left = lax.axis_index("head") == 0
        grad_full = jnp.concatenate(
            [jnp.where(left, mixed_grad, other), jnp.where(left, other, mixed_grad)], axis=1
        )
    else:
        grad_full = lax.all_gather(mixed_grad, "head", axis=1, tiled=True)
    stacks = []
    for g in range(groups):
        own = jnp.stack([keys[:, cut[g]], values[:, cut[g]]])
        stacks.append([own, move(own, inward), move(own, outward), move(own, swapped)])
    grad_attention = lax.dot_general(
        grad_full, out_weight, (((1,), (1,)), ((), ())), preferred_element_type=jnp.float32
    ).astype(jnp.bfloat16)

    atts, gqs, gkvs = [], [], []
    f32 = jnp.float32
    for slabs in stacks:
        slabs[1], grad_attention = lax.optimization_barrier((slabs[1], grad_attention))
        slabs.append(move(slabs[1], swapped))
    for g in range(groups):
        att, gq, own_t, a_t, b_t, po_t, pa_t = attend(
            index, lengths, dilation, queries, grad_attention, stacks[g], g * gh, total, factor, width
        )
        pa_back = move(pa_t, swapped)
        b_back = move(b_t, inward)
        po_back = move(po_t, swapped)
        a_sum = (a_t.astype(f32) + pa_back.astype(f32)).astype(jnp.bfloat16)
        a_sum, att = lax.optimization_barrier((a_sum, att))
        a_back = move(a_sum, outward)
        terms = (own_t, po_back, b_back, a_back)
        gkvs.append(
            [sum(term[i].astype(f32) for term in terms).astype(jnp.bfloat16) for i in range(2)]
        )
        atts.append(att)
        gqs.append(gq)
    attention = jnp.concatenate(atts, axis=1)
    partial = jnp.dot(attention, out_weight, preferred_element_type=f32)
    if sides == 2:
        lo, hi = partial[:, :half], partial[:, half:]
        away = jnp.where(left, hi, lo).astype(jnp.bfloat16)
        came = lax.ppermute(away, "head", [(0, 1), (1, 0)])
        mixed = (jnp.where(left, lo, hi) + came.astype(f32)).astype(jnp.bfloat16)
    else:
        mixed = lax.psum_scatter(
            partial.astype(jnp.bfloat16), "head", scatter_dimension=1, tiled=True
        )
    grad_keys, grad_values = (
        jnp.concatenate([pair[i] for pair in gkvs], axis=1) for i in range(2)
    )
    return mixed, jnp.concatenate(gqs, axis=1), grad_keys, grad_values


def solution(mesh):
    both = P("ctx", "head")
    return jax.shard_map(
        per_device,
        mesh=mesh,
        in_specs=(both, both, both, P("head", None), both, P(), P("head")),
        out_specs=(both, both, both, both),
        check_vma=False,
    )
```

profile of v0, /device:TPU:0, one launch (start us, length us, event | category | flops | bytes accessed | tf_op | source)
XLA Modules:
  0.0 81.6 jit_solution(16641893389574561125)
XLA Ops:
  0.6 3.0 %collective-permute-start.1 = (bf16[128,2048]{1,0:T(8,128)(2,1)}, bf16[128,2048]{1,0:T(8,128)(2,1)S(1)}, u32[]{:S(2)}, u32[]{:S(2)}) collective-permute-start(bf16[128,2048]{1,0:T(8,128)(2,1)} %param.11), channel_id=1, source_target_pairs={{0,1},{1,0},{2,3},{3,2},{4,5},{5,4},{6,7},{7,6},{8,9},{9,8},{10,11... | collective-permute-start | bytes 1572872 | tf_op jit(solution)/shard_map/ppermute | solution.py:129
  3.7 1.1 %pad_maximum_fusion.own_ref = bf16[2,128,1024]{2,1,0:T(8,128)(2,1)S(1)} fusion(bf16[1,128,1024]{2,1,0:T(8,128)(2,1)} %bitcast.10, bf16[1,128,1024]{2,1,0:T(8,128)(2,1)} %bitcast.11), kind=kLoop, calls=%fused_computation.7 | loop fusion | flops 262144 | bytes 1048576 | tf_op jit(solution)/shard_map/stack | solution.py:138
  4.8 3.5 %collective-permute-start.2 = (bf16[2,128,1024]{2,1,0:T(8,128)(2,1)S(1)}, bf16[2,128,1024]{2,1,0:T(8,128)(2,1)S(1)}, u32[]{:S(2)}, u32[]{:S(2)}) collective-permute-start(bf16[2,128,1024]{2,1,0:T(8,128)(2,1)S(1)} %pad_maximum_fusion.own_ref), channel_id=1, source_target_pairs={{6,2},{0,4},{10,6},{4,8},{14,10},{8,12},{18,14},{12,16},{22,18},{1... | collective-permute-start | bytes 1572872 | tf_op jit(solution)/shard_map/ppermute | solution.py:122
  8.3 1.3 %collective-permute-start = (bf16[2,128,1024]{2,1,0:T(8,128)(2,1)S(1)}, bf16[2,128,1024]{2,1,0:T(8,128)(2,1)S(1)}, u32[]{:S(2)}, u32[]{:S(2)}) collective-permute-start(bf16[2,128,1024]{2,1,0:T(8,128)(2,1)S(1)} %pad_maximum_fusion.own_ref), channel_id=1, source_target_pairs={{2,6},{4,0},{6,10},{8,4},{10,14},{12,8},{14,18},{16,12},{18,22},{2... | collective-permute-start | bytes 1572872 | tf_op jit(solution)/shard_map/ppermute | solution.py:122
  9.6 6.2 %collective-permute-done.1 = bf16[128,2048]{1,0:T(8,128)(2,1)S(1)} collective-permute-done((bf16[128,2048]{1,0:T(8,128)(2,1)}, bf16[128,2048]{1,0:T(8,128)(2,1)S(1)}, u32[]{:S(2)}, u32[]{:S(2)}) %collective-permute-start.1) | collective-permute-done | bytes 524320 | tf_op jit(solution)/shard_map/ppermute | solution.py:129
  15.8 1.1 %broadcast_select_fusion.1 = (bf16[128,2048]{1,0:T(8,128)(2,1)S(1)}, bf16[128,2048]{1,0:T(8,128)(2,1)S(1)}) fusion(bf16[128,2048]{1,0:T(8,128)(2,1)} %param.11, bf16[128,2048]{1,0:T(8,128)(2,1)S(1)} %collective-permute-done.1, pred[]{:T(512)S(6)} %eq.3), kind=kLoop, calls=%fused_computation.11 | loop fusion | flops 524288 | bytes 2097153 | tf_op jit(solution)/shard_map/jit(_where)/select_n | solution.py:132
  16.9 7.0 %convolution_convert_fusion.go_ref = bf16[128,1024]{1,0:T(8,128)(2,1)} fusion(bf16[1024,4096]{1,0:T(8,128)(2,1)} %param.10, bf16[128,2048]{1,0:T(8,128)(2,1)S(1)} %get-tuple-element.29, bf16[128,2048]{1,0:T(8,128)(2,1)S(1)} %get-tuple-element.28), kind=kOutput, calls=%fused_computation | convolution fusion | flops 1075970048 | bytes 9699328 | tf_op jit(solution)/shard_map/dot_general | solution.py:140
  23.9 8.0 %collective-permute-start.4 = (bf16[2,128,1024]{2,1,0:T(8,128)(2,1)S(1)}, bf16[2,128,1024]{2,1,0:T(8,128)(2,1)S(1)}, u32[]{:S(2)}, u32[]{:S(2)}) collective-permute-start(bf16[2,128,1024]{2,1,0:T(8,128)(2,1)S(1)} %collective-permute-done.a_ref), channel_id=1, source_target_pairs={{0,2},{2,0},{4,6},{6,4},{8,10},{10,8},{12,14},{14,12},{16,18},{18,... | collective-permute-start | bytes 1572872 | tf_op jit(solution)/shard_map/ppermute | solution.py:122
  31.9 1.5 %collective-permute-done.4.pa_ref = bf16[2,128,1024]{2,1,0:T(8,128)(2,1)S(1)} collective-permute-done((bf16[2,128,1024]{2,1,0:T(8,128)(2,1)S(1)}, bf16[2,128,1024]{2,1,0:T(8,128)(2,1)S(1)}, u32[]{:S(2)}, u32[]{:S(2)}) %collective-permute-start.4) | collective-permute-done | bytes 524320 | tf_op jit(solution)/shard_map/ppermute | solution.py:122
  33.5 0.8 copy-done.7
  34.3 10.0 %shard_map.102 = (bf16[128,1024]{1,0:T(8,128)(2,1)}, bf16[128,1024]{1,0:T(8,128)(2,1)}, bf16[2,128,1024]{2,1,0:T(8,128)(2,1)}, bf16[2,128,1024]{2,1,0:T(8,128)(2...) custom-call(s32[1]{0:T(128)} %bitcast.index_ref, s32[16]{0:T(128)} %length_ref.1, ...), custom_call_target="tpu_custom_call" | custom-call | flops 8053063680 | bytes 6291456 | tf_op jit(solution)/shard_map/pallas_call | solution.py:88
  44.3 0.4 collective-permute-start.5
  44.8 1.7 %collective-permute-done.5 = bf16[2,128,1024]{2,1,0:T(8,128)(2,1)S(1)} collective-permute-done((bf16[2,128,1024]{2,1,0:T(8,128)(2,1)}, bf16[2,128,1024]{2,1,0:T(8,128)(2,1)S(1)}, u32[]{:S(2)}, u32[]{:S(2)}) %collective-permute-start.5) | collective-permute-done | bytes 524320 | tf_op jit(solution)/shard_map/ppermute | solution.py:122
  46.5 1.2 %add_convert_fusion.1 = bf16[2,128,1024]{2,1,0:T(8,128)(2,1)S(1)} fusion(bf16[2,128,1024]{2,1,0:T(8,128)(2,1)S(1)} %collective-permute-done.5, bf16[2,128,1024]{2,1,0:T(8,128)(2,1)} %get-tuple-element.17), kind=kLoop, calls=%fused_computation.6 | loop fusion | flops 1048576 | bytes 1572864 | tf_op jit(solution)/shard_map/convert_element_type | solution.py:156
  47.8 4.8 %fusion.6 = f32[128,4096]{1,0:T(8,128)S(1)} fusion(bf16[128,1024]{1,0:T(8,128)(2,1)} %get-tuple-element.20, bf16[1024,4096]{1,0:T(8,128)(2,1)} %param.10), kind=kOutput, calls=%fused_computation.15 | convolution fusion | flops 1073741824 | bytes 10747904 | tf_op jit(solution)/shard_map/dot_general | solution.py:166
  52.6 0.1 select_convert_fusion
  52.7 0.6 collective-permute-start.6
  53.3 0.1 collective-permute-start.7
  53.4 1.3 %collective-permute-start.8 = (bf16[2,128,1024]{2,1,0:T(8,128)(2,1)S(1)}, bf16[2,128,1024]{2,1,0:T(8,128)(2,1)S(1)}, u32[]{:S(2)}, u32[]{:S(2)}) collective-permute-start(bf16[2,128,1024]{2,1,0:T(8,128)(2,1)S(1)} %copy-done.5), channel_id=1, source_target_pairs={{2,6},{4,0},{6,10},{8,4},{10,14},{12,8},{14,18},{16,12},{18,22},{2... | collective-permute-start | bytes 1572872 | tf_op jit(solution)/shard_map/ppermute | solution.py:122
  54.7 4.8 %collective-permute-start.9 = (bf16[2,128,1024]{2,1,0:T(8,128)(2,1)S(1)}, bf16[2,128,1024]{2,1,0:T(8,128)(2,1)S(1)}, u32[]{:S(2)}, u32[]{:S(2)}) collective-permute-start(bf16[2,128,1024]{2,1,0:T(8,128)(2,1)S(1)} %add_convert_fusion.1), channel_id=1, source_target_pairs={{6,2},{0,4},{10,6},{4,8},{14,10},{8,12},{18,14},{12,16},{22,18},{1... | collective-permute-start | bytes 1572872 | tf_op jit(solution)/shard_map/ppermute | solution.py:122
  59.5 7.5 %collective-permute-done.6 = bf16[128,2048]{1,0:T(8,128)(2,1)S(1)} collective-permute-done((bf16[128,2048]{1,0:T(8,128)(2,1)S(1)}, bf16[128,2048]{1,0:T(8,128)(2,1)S(1)}, u32[]{:S(2)}, u32[]{:S(2)}) %collective-permute-start.6) | collective-permute-done | bytes 524320 | tf_op jit(solution)/shard_map/ppermute | solution.py:170
  67.0 1.0 %add_convert_fusion = bf16[128,2048]{1,0:T(8,128)(2,1)} fusion(bf16[128,2048]{1,0:T(8,128)(2,1)S(1)} %collective-permute-done.6, f32[128,4096]{1,0:T(8,128)S(1)} %fusion.6, pred[]{:T(512)S(6)} %eq.3), kind=kLoop, calls=%fused_computation.4 | loop fusion | flops 1048576 | bytes 3145729 | tf_op jit(solution)/shard_map/convert_element_type | solution.py:171
  68.0 12.5 %collective-permute-done.9 = bf16[2,128,1024]{2,1,0:T(8,128)(2,1)S(1)} collective-permute-done((bf16[2,128,1024]{2,1,0:T(8,128)(2,1)S(1)}, bf16[2,128,1024]{2,1,0:T(8,128)(2,1)S(1)}, u32[]{:S(2)}, u32[]{:S(2)}) %collective-permute-start.9) | collective-permute-done | bytes 524320 | tf_op jit(solution)/shard_map/ppermute | solution.py:122
  80.5 1.1 %fusion.4 = (bf16[128,1024]{1,0:T(8,128)(2,1)}, bf16[128,1024]{1,0:T(8,128)(2,1)}) fusion(bf16[2,128,1024]{2,1,0:T(8,128)(2,1)S(1)} %collective-permute-done.9, bf16[2,128,1024]{2,1,0:T(8,128)(2,1)S(1)} %collective-permute-done.8, bf16[2,128,1024]{2,1,0:T(8,128)(2,1)S(1)} %collective-permute-done.7, bf16[2,128,1024]{2,1,0:T(8,128)(2,1)S(1)} %copy-done), kind=kLoop, calls=%fused_computation.13 | loop fusion | flops 2097152 | bytes 2621440 | tf_op jit(solution)/shard_map/add | solution.py:161
  (21 shorter events, 0.1 us)
Async XLA Ops:
  0.6 15.2 %collective-permute-start.1 = (bf16[128,2048]{1,0:T(8,128)(2,1)}, bf16[128,2048]{1,0:T(8,128)(2,1)S(1)}, u32[]{:S(2)}, u32[]{:S(2)}) collective-permute-start(bf16[128,2048]{1,0:T(8,128)(2,1)} %param.11), channel_id=1, source_target_pairs={{0,1},{1,0},{2,3},{3,2},{4,5},{5,4},{6,7},{7,6},{8,9},{9,8},{10,11... | collective-permute-start | bytes 1572872 | tf_op jit(solution)/shard_map/ppermute | solution.py:129
  4.7 28.7 %copy-start.1 = (bf16[2,128,1024]{2,1,0:T(8,128)(2,1)}, bf16[2,128,1024]{2,1,0:T(8,128)(2,1)S(1)}, u32[]{:S(2)}) copy-start(bf16[2,128,1024]{2,1,0:T(8,128)(2,1)S(1)} %pad_maximum_fusion.own_ref) | copy-start | bytes 1572868
  4.8 27.2 %collective-permute-start.3 = (bf16[2,128,1024]{2,1,0:T(8,128)(2,1)S(1)}, bf16[2,128,1024]{2,1,0:T(8,128)(2,1)S(1)}, u32[]{:S(2)}, u32[]{:S(2)}) collective-permute-start(bf16[2,128,1024]{2,1,0:T(8,128)(2,1)S(1)} %pad_maximum_fusion.own_ref), channel_id=1, source_target_pairs={{0,2},{2,0},{4,6},{6,4},{8,10},{10,8},{12,14},{14,12},{16,18},{18,... | collective-permute-start | bytes 1572872 | tf_op jit(solution)/shard_map/ppermute | solution.py:122
  4.8 27.1 %collective-permute-start.2 = (bf16[2,128,1024]{2,1,0:T(8,128)(2,1)S(1)}, bf16[2,128,1024]{2,1,0:T(8,128)(2,1)S(1)}, u32[]{:S(2)}, u32[]{:S(2)}) collective-permute-start(bf16[2,128,1024]{2,1,0:T(8,128)(2,1)S(1)} %pad_maximum_fusion.own_ref), channel_id=1, source_target_pairs={{6,2},{0,4},{10,6},{4,8},{14,10},{8,12},{18,14},{12,16},{22,18},{1... | collective-permute-start | bytes 1572872 | tf_op jit(solution)/shard_map/ppermute | solution.py:122
  8.3 15.6 %collective-permute-start = (bf16[2,128,1024]{2,1,0:T(8,128)(2,1)S(1)}, bf16[2,128,1024]{2,1,0:T(8,128)(2,1)S(1)}, u32[]{:S(2)}, u32[]{:S(2)}) collective-permute-start(bf16[2,128,1024]{2,1,0:T(8,128)(2,1)S(1)} %pad_maximum_fusion.own_ref), channel_id=1, source_target_pairs={{2,6},{4,0},{6,10},{8,4},{10,14},{12,8},{14,18},{16,12},{18,22},{2... | collective-permute-start | bytes 1572872 | tf_op jit(solution)/shard_map/ppermute | solution.py:122
  23.9 9.6 %copy-start.4 = (bf16[2,128,1024]{2,1,0:T(8,128)(2,1)}, bf16[2,128,1024]{2,1,0:T(8,128)(2,1)S(1)}, u32[]{:S(2)}) copy-start(bf16[2,128,1024]{2,1,0:T(8,128)(2,1)S(1)} %collective-permute-done.a_ref) | copy-start | bytes 1572868
  23.9 9.6 %collective-permute-start.4 = (bf16[2,128,1024]{2,1,0:T(8,128)(2,1)S(1)}, bf16[2,128,1024]{2,1,0:T(8,128)(2,1)S(1)}, u32[]{:S(2)}, u32[]{:S(2)}) collective-permute-start(bf16[2,128,1024]{2,1,0:T(8,128)(2,1)S(1)} %collective-permute-done.a_ref), channel_id=1, source_target_pairs={{0,2},{2,0},{4,6},{6,4},{8,10},{10,8},{12,14},{14,12},{16,18},{18,... | collective-permute-start | bytes 1572872 | tf_op jit(solution)/shard_map/ppermute | solution.py:122
  31.9 1.5 %copy-start.2 = (bf16[2,128,1024]{2,1,0:T(8,128)(2,1)}, bf16[2,128,1024]{2,1,0:T(8,128)(2,1)S(1)}, u32[]{:S(2)}) copy-start(bf16[2,128,1024]{2,1,0:T(8,128)(2,1)S(1)} %collective-permute-done.3.po_ref) | copy-start | bytes 1572868
  31.9 1.5 %copy-start.3 = (bf16[2,128,1024]{2,1,0:T(8,128)(2,1)}, bf16[2,128,1024]{2,1,0:T(8,128)(2,1)S(1)}, u32[]{:S(2)}) copy-start(bf16[2,128,1024]{2,1,0:T(8,128)(2,1)S(1)} %collective-permute-done.2.b_ref) | copy-start | bytes 1572868
  33.5 0.8 %copy-start.7 = (bf16[2,128,1024]{2,1,0:T(8,128)(2,1)}, bf16[2,128,1024]{2,1,0:T(8,128)(2,1)S(1)}, u32[]{:S(2)}) copy-start(bf16[2,128,1024]{2,1,0:T(8,128)(2,1)S(1)} %collective-permute-done.4.pa_ref) | copy-start | bytes 1572868
  44.3 2.2 %collective-permute-start.5 = (bf16[2,128,1024]{2,1,0:T(8,128)(2,1)}, bf16[2,128,1024]{2,1,0:T(8,128)(2,1)S(1)}, u32[]{:S(2)}, u32[]{:S(2)}) collective-permute-start(bf16[2,128,1024]{2,1,0:T(8,128)(2,1)} %get-tuple-element.18), channel_id=1, source_target_pairs={{0,2},{2,0},{4,6},{6,4},{8,10},{10,8},{12,14},{14,12},{16,18},{18,... | collective-permute-start | bytes 1572872 | tf_op jit(solution)/shard_map/ppermute | solution.py:122
  47.8 5.6 %copy-start.6 = (bf16[2,128,1024]{2,1,0:T(8,128)(2,1)S(1)}, bf16[2,128,1024]{2,1,0:T(8,128)(2,1)}, u32[]{:S(2)}) copy-start(bf16[2,128,1024]{2,1,0:T(8,128)(2,1)} %get-tuple-element.23) | copy-start | bytes 1572868
  47.8 5.7 %copy-start.5 = (bf16[2,128,1024]{2,1,0:T(8,128)(2,1)S(1)}, bf16[2,128,1024]{2,1,0:T(8,128)(2,1)}, u32[]{:S(2)}) copy-start(bf16[2,128,1024]{2,1,0:T(8,128)(2,1)} %get-tuple-element.24) | copy-start | bytes 1572868
  47.8 32.7 %copy-start = (bf16[2,128,1024]{2,1,0:T(8,128)(2,1)S(1)}, bf16[2,128,1024]{2,1,0:T(8,128)(2,1)}, u32[]{:S(2)}) copy-start(bf16[2,128,1024]{2,1,0:T(8,128)(2,1)} %get-tuple-element.22) | copy-start | bytes 1572868
  52.7 14.3 %collective-permute-start.6 = (bf16[128,2048]{1,0:T(8,128)(2,1)S(1)}, bf16[128,2048]{1,0:T(8,128)(2,1)S(1)}, u32[]{:S(2)}, u32[]{:S(2)}) collective-permute-start(bf16[128,2048]{1,0:T(8,128)(2,1)S(1)} %select_convert_fusion), channel_id=1, source_target_pairs={{0,1},{1,0},{2,3},{3,2},{4,5},{5,4},{6,7},{7,6},{8,9},{9,8},{10,11... | collective-permute-start | bytes 1572872 | tf_op jit(solution)/shard_map/ppermute | solution.py:170
  53.3 14.7 %collective-permute-start.7 = (bf16[2,128,1024]{2,1,0:T(8,128)(2,1)S(1)}, bf16[2,128,1024]{2,1,0:T(8,128)(2,1)S(1)}, u32[]{:S(2)}, u32[]{:S(2)}) collective-permute-start(bf16[2,128,1024]{2,1,0:T(8,128)(2,1)S(1)} %copy-done.6), channel_id=1, source_target_pairs={{0,2},{2,0},{4,6},{6,4},{8,10},{10,8},{12,14},{14,12},{16,18},{18,... | collective-permute-start | bytes 1572872 | tf_op jit(solution)/shard_map/ppermute | solution.py:122
  53.4 14.6 %collective-permute-start.8 = (bf16[2,128,1024]{2,1,0:T(8,128)(2,1)S(1)}, bf16[2,128,1024]{2,1,0:T(8,128)(2,1)S(1)}, u32[]{:S(2)}, u32[]{:S(2)}) collective-permute-start(bf16[2,128,1024]{2,1,0:T(8,128)(2,1)S(1)} %copy-done.5), channel_id=1, source_target_pairs={{2,6},{4,0},{6,10},{8,4},{10,14},{12,8},{14,18},{16,12},{18,22},{2... | collective-permute-start | bytes 1572872 | tf_op jit(solution)/shard_map/ppermute | solution.py:122
  54.7 25.8 %collective-permute-start.9 = (bf16[2,128,1024]{2,1,0:T(8,128)(2,1)S(1)}, bf16[2,128,1024]{2,1,0:T(8,128)(2,1)S(1)}, u32[]{:S(2)}, u32[]{:S(2)}) collective-permute-start(bf16[2,128,1024]{2,1,0:T(8,128)(2,1)S(1)} %add_convert_fusion.1), channel_id=1, source_target_pairs={{6,2},{0,4},{10,6},{4,8},{14,10},{8,12},{18,14},{12,16},{22,18},{1... | collective-permute-start | bytes 1572872 | tf_op jit(solution)/shard_map/ppermute | solution.py:122
where the time goes:
time: 82.5 us; the launch traced here: 81.6 us
  waiting for transfers between devices  29.5 us (36%)
  starting transfers between devices  23 us (28%)
  matrix products  11.8 us (14%)
  Pallas kernels  10 us (12%)
  other arithmetic  5.68 us (7%)
  local copies, waits for them, and re-layouts  0.83 us (1%)
    ppermute x8, starting transfers between devices, move(): return lax.ppermute(x, 'ctx', pairs)  19.4 us
    ppermute x8, waiting for transfers between devices, move(): return lax.ppermute(x, 'ctx', pairs)  15.8 us
    pallas_call x1, Pallas kernels, attend(): pl.pallas_call(functools.partial(attend_kernel, rows, total, factor, firs...  10 us
    ppermute x1, waiting for transfers between devices, per_device(): came = lax.ppermute(away, 'head', [(0, 1), (1, 0)])  7.52 us
    dot_general x1, matrix products, per_device(): lax.dot_general(grad_full, out_weight, (((1,), (1,)), ((), ())), preferre...  6.97 us
    ppermute x1, waiting for transfers between devices, per_device(): other = lax.ppermute(mixed_grad, 'head', [(0, 1), (1, 0)])  6.19 us
    dot_general x1, matrix products, per_device(): partial = jnp.dot(attention, out_weight, preferred_element_type=f32)  4.84 us
    ppermute x1, starting transfers between devices, per_device(): other = lax.ppermute(mixed_grad, 'head', [(0, 1), (1, 0)])  3.03 us
  transfers between devices with their start and end apart: 10, of which 5 were waited for; matrix products, arithmetic and copies ran while one was open for 12% of the time, Pallas kernels for 0%

commit v1 on v0

--- a/solution.py
+++ b/solution.py
@@ -10,6 +10,538 @@
 MAXD = 8
 FAR = 1e6
 NEG = -1e30
+HEAD_WIDTH = 128
+
+GROUP = 4
+NT = (((1,), (1,)), ((), ()))
+TN = (((0,), (0,)), ((), ()))
+F32 = jnp.float32
+BF16 = jnp.bfloat16
+MESH_ID = pl.DeviceIdType.MESH
+
+
+def fused_kernel(
+    groups, length_hbm, dilation_hbm, q_ref, k_ref, v_ref, w_ref, mg_ref,
+    mixed_ref, gq_ref, gk_ref, gv_ref,
+    w_own, w_oth, mg_own, mg_oth, kv, qs, gos, go_acc, go_bf, att_my, att_in,
+    part_send, part_recv, part_own, probs, spaced, bounds, terms,
+    slopes, halo_send, halo_recv, dq, dkv, mixed_out, length_ref, dilation_ref,
+    int_sem, w_sem, mg_sem, own_sem, x_recv, kv_recv, q_recv, halo_kv, go_recv, att_recv,
+    p_recv, h_recv, out_recv, mixed_sem, sent, sent_fwd, sent_bwd,
+):
+    rows = q_ref.shape[0]
+    width = HEAD_WIDTH
+    heads = q_ref.shape[1] // GROUP // width
+    feats = mg_ref.shape[1]
+    chunks = mg_oth.shape[0]
+    step = feats // chunks
+    window = kv.shape[2] - 2 * rows
+    block = 2 * rows
+    halo = 2 * rows
+    factor = width ** (-0.5)
+    scope = jax.named_scope
+
+    c = lax.axis_index("ctx")
+    side = lax.axis_index("head")
+    g = c // GROUP
+    r = c % GROUP
+    y = r // 2
+    core = r % 2
+    peers = (r, r + 1 - 2 * core, r + 2 - 4 * y, (GROUP - 1) - r)
+    base = g * GROUP
+    ahead = 2 * y - 1
+    has_fwd = (g + ahead >= 0) & (g + ahead < groups)
+    has_bwd = (g - ahead >= 0) & (g - ahead < groups)
+    fwd_id = {"ctx": c + GROUP * ahead}
+    bwd_id = {"ctx": c - GROUP * ahead}
+    x_id = {"head": 1 - side}
+
+    def peer_id(o):
+        return {"ctx": base + peers[o]}
+
+    def lanes(i, h):
+        return pl.ds(pl.multiple_of((i * heads + h) * width, width), width)
+
+    def slab(i, first=0):
+        return pl.ds(pl.multiple_of(first + i * rows, rows), rows)
+
+    def arrived(ref, sem):
+        pltpu.make_async_copy(ref, ref, sem).wait()
+
+    def remote(src, dst, send, recv, device):
+        return pltpu.make_async_remote_copy(
+            src_ref=src, dst_ref=dst, send_sem=send, recv_sem=recv,
+            device_id=device, device_id_type=MESH_ID,
+        )
+
+    integers = (
+        pltpu.make_async_copy(length_hbm, length_ref, int_sem.at[0]),
+        pltpu.make_async_copy(dilation_hbm, dilation_ref, int_sem.at[1]),
+    )
+    for copy in integers:
+        copy.start()
+
+    barrier = pltpu.get_barrier_semaphore()
+    for o in (1, 2, 3):
+        pl.semaphore_signal(barrier, inc=1, device_id=peer_id(o), device_id_type=MESH_ID)
+    pl.semaphore_signal(barrier, inc=1, device_id=x_id, device_id_type=MESH_ID)
+
+    @pl.when(has_fwd)
+    def _():
+        pl.semaphore_signal(barrier, inc=1, device_id=fwd_id, device_id_type=MESH_ID)
+
+    @pl.when(has_bwd)
+    def _():
+        pl.semaphore_signal(barrier, inc=1, device_id=bwd_id, device_id_type=MESH_ID)
+
+    def w_copy(half):
+        where = side if half == 0 else 1 - side
+        return pltpu.make_async_copy(
+            w_ref.at[:, pl.ds(pl.multiple_of(where * feats, feats), feats)],
+            (w_own, w_oth)[half], w_sem.at[half],
+        )
+
+    def part(n):
+        return slice(n * step, (n + 1) * step)
+
+    def in_place(t, h):
+        return kv.at[h, t, slab(r, halo), :] if t < 2 else qs.at[h, slab(r), :]
+
+    def own(t, h):
+        source = (k_ref, v_ref, q_ref)[t].at[:, lanes(r, h)]
+        return pltpu.make_async_copy(source, in_place(t, h), own_sem if t < 2 else q_recv.at[h])
+
+    mg_copy = pltpu.make_async_copy(mg_ref, mg_own, mg_sem)
+    for h in range(heads):
+        own(0, h).start()
+        own(1, h).start()
+    mg_copy.start()
+    w_copy(0).start()
+    for h in range(heads):
+        own(2, h).start()
+
+    neighbours = has_fwd.astype(jnp.int32) + has_bwd.astype(jnp.int32)
+    with scope("barrier"):
+        pl.semaphore_wait(barrier, GROUP + neighbours)
+
+    def x_copy(n):
+        return remote(
+            mg_ref.at[:, pl.ds(n * step, step)], mg_oth.at[n], sent, x_recv.at[n], x_id
+        )
+
+    def in_copy(t, o, h):
+        source = (k_ref, v_ref, q_ref)[t].at[:, lanes(peers[o], h)]
+        recv = kv_recv.at[o - 1, h] if t < 2 else q_recv.at[h]
+        return remote(source, in_place(t, h), sent, recv, peer_id(o))
+
+    with scope("send"):
+        x_copy(0).start()
+        for h in range(heads):
+            for t, o in ((0, 2), (1, 2), (0, 3), (1, 3), (0, 1), (1, 1)):
+                in_copy(t, o, h).start()
+        for n in range(1, chunks):
+            x_copy(n).start()
+        for h in range(heads):
+            for o in (2, 3, 1):
+                in_copy(2, o, h).start()
+        w_copy(1).start()
+
+    def relay(o, h):
+        to = ahead if o < 2 else -ahead
+        src_row = halo + peers[o] * rows
+        dst_row = src_row - to * (GROUP * rows)
+        return remote(
+            kv.at[h, :, pl.ds(pl.multiple_of(src_row, rows), rows), :],
+            kv.at[h, :, pl.ds(pl.multiple_of(dst_row, rows), rows), :],
+            sent_fwd if o < 2 else sent_bwd, halo_kv.at[o // 2, h], fwd_id if o < 2 else bwd_id,
+        )
+
+    def pass_on(o, h):
+        if o > 0:
+            arrived(kv.at[h, :, slab(peers[o], halo), :], kv_recv.at[o - 1, h])
+
+        @pl.when(has_fwd if o < 2 else has_bwd)
+        def _():
+            relay(o, h).start()
+
+    near_row = pl.multiple_of((halo + GROUP * rows) * (1 - y), halo)
+    far_row = pl.multiple_of((halo + GROUP * rows) * y, halo)
+
+    @pl.when(jnp.logical_not(has_bwd))
+    def _():
+        for h in range(heads):
+            kv[h, :, pl.ds(near_row, halo), :] = jnp.zeros((2, halo, width), BF16)
+        halo_recv[1] = jnp.zeros(halo_recv.shape[1:], BF16)
+
+    @pl.when(jnp.logical_not(has_fwd))
+    def _():
+        for h in range(heads):
+            kv[h, :, pl.ds(far_row, halo), :] = jnp.zeros((2, halo, width), BF16)
+        halo_recv[0] = jnp.zeros(halo_recv.shape[1:], BF16)
+
+    arrived(kv.at[:, :, slab(r, halo), :], own_sem)
+    for h in range(heads):
+        pass_on(0, h)
+
+    for copy in integers:
+        copy.wait()
+    with scope("masks"):
+        rel = lax.broadcasted_iota(jnp.int32, (window, block), 0) - halo
+        rel = rel - lax.broadcasted_iota(jnp.int32, (window, block), 1)
+        relf = rel.astype(F32)
+        for h in range(heads):
+            spacing = jnp.full((1, block), dilation_ref[r * heads + h], jnp.int32)
+            inv = 1.0 / spacing.astype(F32)
+            steps = relf * inv
+            whole = jnp.floor(steps + 0.5)
+            spaced[h] = jnp.where(jnp.abs(steps - whole) < 0.01, rel, 1 << 24)
+        for b in range(2):
+            qpos = base * rows + b * block + lax.broadcasted_iota(jnp.int32, (1, block), 1)
+            start = jnp.zeros((1, block), jnp.int32)
+            stop = jnp.full((1, block), 1 << 24, jnp.int32)
+            end = jnp.int32(0)
+            for n in range(length_ref.shape[0]):
+                end = end + length_ref[n]
+                past = qpos >= end
+                start = jnp.where(past, jnp.maximum(start, end), start)
+                stop = jnp.where(past, stop, jnp.minimum(stop, end))
+            for h in range(heads):
+                reach = jnp.full((1, block), HALF * dilation_ref[r * heads + h], jnp.int32)
+                bounds[b, h, 0:1, :] = jnp.maximum(start - qpos, -reach)
+                bounds[b, h, 1:2, :] = jnp.minimum(stop - 1 - qpos, reach)
+
+    def go_step(mg, weight, first):
+        term = lax.dot_general(mg, weight, NT, preferred_element_type=F32)
+        if first:
+            go_acc[...] = term
+        else:
+            go_acc[...] += term
+
+    mg_copy.wait()
+    w_copy(0).wait()
+    for n in range(chunks):
+        with scope("go_own"):
+            go_step(mg_own[:, part(n)], w_own[:, part(n)], n == 0)
+
+    def go_far(n):
+        if n == 0:
+            w_copy(1).wait()
+        with scope("wait_x"):
+            x_copy(n).wait_recv()
+        with scope("go_far"):
+            go_step(mg_oth[n], w_oth[:, part(n)], False)
+
+    with scope("wait_kv"):
+        for h in range(heads):
+            pass_on(1, h)
+        for h in range(heads):
+            for o in (2, 3):
+                pass_on(o, h)
+
+    def at_rows(i):
+        return pl.multiple_of((1 - y) * block if i == 0 else y * block, block)
+
+    def forward(i, h):
+        row0 = at_rows(i)
+        b = 1 - y if i == 0 else y
+        k = kv[h, 0, pl.ds(row0, window), :]
+        v = kv[h, 1, pl.ds(row0, window), :]
+        q = qs[h, pl.ds(row0, block), :]
+        s = lax.dot_general(k, q, NT, preferred_element_type=F32)
+        rel = spaced[h]
+        lo = bounds[b, h, 0:1, :]
+        hi = bounds[b, h, 1:2, :]
+        s = jnp.where((rel >= lo) & (rel <= hi), s, NEG)
+        top = jnp.max(s, axis=0, keepdims=True)
+        e = jnp.exp((s - top) * factor)
+        w = e * (1.0 / jnp.sum(e, axis=0, keepdims=True))
+        p = w.astype(BF16)
+        probs[i, h] = p
+        att = lax.dot_general(p, v, TN, preferred_element_type=F32)
+        att_my[h, pl.ds(row0, block), :] = att.astype(BF16)
+
+    def att_copy(o, h):
+        return remote(
+            att_my.at[h, slab(peers[o]), :], att_in.at[:, lanes(r, h)],
+            sent, att_recv, peer_id(o),
+        )
+
+    def att_local(h):
+        return pltpu.make_async_copy(
+            att_my.at[h, slab(r), :], att_in.at[:, lanes(r, h)], att_recv
+        )
+
+    def near_block(h):
+        with scope("wait_q"):
+            arrived(qs.at[h], q_recv.at[h])
+
+        @pl.when(has_bwd)
+        def _():
+            with scope("wait_near"):
+                arrived(kv.at[h, :, pl.ds(near_row, halo), :], halo_kv.at[0, h])
+
+        with scope("forward"):
+            forward(0, h)
+        for o in (2, 3):
+            att_copy(o, h).start()
+
+    def far_block(h):
+        @pl.when(has_fwd)
+        def _():
+            with scope("wait_far"):
+                arrived(kv.at[h, :, pl.ds(far_row, halo), :], halo_kv.at[1, h])
+
+        with scope("forward"):
+            forward(1, h)
+        att_copy(1, h).start()
+        att_local(h).start()
+
+    go_far(0)
+    for h in range(heads):
+        near_block(h)
+        far_block(h)
+    for n in range(1, chunks):
+        go_far(n)
+
+    def go_copy(o, h):
+        return remote(
+            go_bf.at[:, lanes(peers[o], h)], gos.at[h, slab(r), :],
+            sent, go_recv.at[h], peer_id(o),
+        )
+
+    def go_local(h):
+        return pltpu.make_async_copy(go_bf.at[:, lanes(r, h)], gos.at[h, slab(r), :], go_recv.at[h])
+
+    go_bf[...] = go_acc[...].astype(BF16)
+    for h in range(heads):
+        for o in (2, 3, 1):
+            go_copy(o, h).start()
+        go_local(h).start()
+
+    with scope("wait_att"):
+        arrived(att_in, att_recv)
+
+    def p_copy(n):
+        return remote(part_send.at[n], part_recv.at[n], sent, p_recv.at[n], x_id)
+
+    for n in range(chunks):
+        with scope("proj_far"):
+            term = jnp.dot(att_in[...], w_oth[:, part(n)], preferred_element_type=F32)
+            part_send[n] = term.astype(BF16)
+        p_copy(n).start()
+
+    with scope("proj_own"):
+        for n in range(chunks):
+            part_own[n] = jnp.dot(att_in[...], w_own[:, part(n)], preferred_element_type=F32)
+
+    def edge_rows(i):
+        return pl.ds(pl.multiple_of(2 * at_rows(i), block), block)
+
+    def edge_values(i, h):
+        go = gos[h, pl.ds(at_rows(i), block), :]
+        dv = jnp.dot(probs[i, h, edge_rows(i), :], go, preferred_element_type=F32)
+        halo_send[i, h, 1] = dv.astype(BF16)
+
+    def edge_keys(i, h):
+        row0 = at_rows(i)
+        v = kv[h, 1, pl.ds(row0, window), :]
+        q = qs[h, pl.ds(row0, block), :]
+        go = gos[h, pl.ds(row0, block), :]
+        gp = lax.dot_general(v, go, NT, preferred_element_type=F32)
+        w = probs[i, h].astype(F32)
+        delta = jnp.sum(w * gp, axis=0, keepdims=True)
+        slopes[i, h] = (w * (gp - delta)).astype(BF16)
+        dk = jnp.dot(slopes[i, h, edge_rows(i), :], q, preferred_element_type=F32) * factor
+        halo_send[i, h, 0] = dk.astype(BF16)
+
+    def query_terms(i, h):
+        row0 = at_rows(i)
+        k = kv[h, 0, pl.ds(row0, window), :]
+        gq = lax.dot_general(slopes[i, h], k, TN, preferred_element_type=F32) * factor
+        dq[h, pl.ds(row0, block), :] = gq.astype(BF16)
+
+    def inner_terms(i, h):
+        row0 = at_rows(i)
+        q = qs[h, pl.ds(row0, block), :]
+        go = gos[h, pl.ds(row0, block), :]
+        inner = pl.ds(pl.multiple_of(halo - row0, block), 2 * block)
+        terms[i, h, 0] = jnp.dot(slopes[i, h, inner, :], q, preferred_element_type=F32) * factor
+        terms[i, h, 1] = jnp.dot(probs[i, h, inner, :], go, preferred_element_type=F32)
+
+    def h_copy(i, h, t):
+        return remote(
+            halo_send.at[i, h, t], halo_recv.at[i, h, t], sent_bwd if i == 0 else sent_fwd,
+            h_recv.at[i, h, t], bwd_id if i == 0 else fwd_id,
+        )
+
+    results = (gq_ref, gk_ref, gv_ref)
+
+    def out_copy(t, o, h):
+        source = dq.at[h] if t == 0 else dkv.at[h, t - 1]
+        return remote(
+            source.at[slab(peers[o]), :], results[t].at[:, lanes(r, h)],
+            sent, out_recv.at[t], peer_id(o),
+        )
+
+    def out_local(t, h):
+        source = dq.at[h] if t == 0 else dkv.at[h, t - 1]
+        return pltpu.make_async_copy(
+            source.at[slab(r), :], results[t].at[:, lanes(r, h)], out_recv.at[t]
+        )
+
+    def sums(t, h):
+        @pl.when(has_fwd)
+        def _():
+            with scope("wait_h0"):
+                arrived(halo_recv.at[0, h, t], h_recv.at[0, h, t])
+
+        @pl.when(has_bwd)
+        def _():
+            with scope("wait_h1"):
+                arrived(halo_recv.at[1, h, t], h_recv.at[1, h, t])
+
+        with scope("sums"):
+            for i in range(2):
+                half = pl.multiple_of(y * block if i == 0 else (1 - y) * block, block)
+                out = pl.ds(half, block)
+                total = terms[0, h, t, out, :] + terms[1, h, t, out, :]
+                total = total + halo_recv[i, h, t].astype(F32)
+                dkv[h, t, out, :] = total.astype(BF16)
+        for o in (2, 3, 1):
+            out_copy(1 + t, o, h).start()
+        out_local(1 + t, h).start()
+
+    def send_edge(t, i, h):
+        with scope("edge"):
+            (edge_keys, edge_values)[t](i, h)
+
+        @pl.when(has_bwd if i == 0 else has_fwd)
+        def _():
+            h_copy(i, h, t).start()
+
+    for h in range(heads):
+        with scope("wait_go"):
+            arrived(gos.at[h], go_recv.at[h])
+        for i in range(2):
+            send_edge(1, i, h)
+        for i in range(2):
+            send_edge(0, i, h)
+            if h > 0:
+                sums(1 - i, h - 1)
+            with scope("query"):
+                query_terms(i, h)
+            if i == 0:
+                out_copy(0, 2, h).start()
+                out_copy(0, 3, h).start()
+            else:
+                out_copy(0, 1, h).start()
+                out_local(0, h).start()
+        with scope("inner"):
+            for i in range(2):
+                inner_terms(i, h)
+    for t in (1, 0):
+        sums(t, heads - 1)
+
+    def mixed_copy(n):
+        return pltpu.make_async_copy(
+            mixed_out.at[n], mixed_ref.at[:, part(n)], mixed_sem
+        )
+
+    for n in range(chunks):
+        with scope("wait_part"):
+            p_copy(n).wait_recv()
+        with scope("mixed"):
+            total = part_own[n] + part_recv[n].astype(F32)
+            mixed_out[n] = total.astype(BF16)
+        mixed_copy(n).start()
+
+    far_sends = (3 + 1 + 1 + 3) * (GROUP - 1) * rows * heads * width
+    sent_rows = (far_sends + 2 * rows * feats) // feats
+    arrived(w_own.at[pl.ds(0, sent_rows), :], sent)
+    side_rows = (2 * 2 * rows + 2 * halo) * heads * width // feats
+
+    @pl.when(has_fwd)
+    def _():
+        arrived(w_own.at[pl.ds(0, side_rows), :], sent_fwd)
+
+    @pl.when(has_bwd)
+    def _():
+        arrived(w_own.at[pl.ds(0, side_rows), :], sent_bwd)
+
+    with scope("end"):
+        for t in range(3):
+            arrived(results[t], out_recv.at[t])
+        arrived(mixed_ref, mixed_sem)
+
+
+def store_kernel(*refs):
+    count = (len(refs) - 1) // 2
+    copies = [
+        pltpu.make_async_copy(refs[i], refs[count + i], refs[-1].at[i]) for i in range(count)
+    ]
+    for copy in copies:
+        copy.start()
+    for copy in copies:
+        copy.wait()
+
+
+def store(arrays):
+    place = pl.BlockSpec(memory_space=pltpu.HBM)
+    return pl.pallas_call(
+        store_kernel,
+        in_specs=[pl.BlockSpec(memory_space=pltpu.VMEM)] * len(arrays),
+        out_specs=[place] * len(arrays),
+        out_shape=[jax.ShapeDtypeStruct(a.shape, a.dtype) for a in arrays],
+        scratch_shapes=[pltpu.SemaphoreType.DMA((len(arrays),))],
+        compiler_params=pltpu.CompilerParams(vmem_limit_bytes=4 * 1024 * 1024),
+    )(*arrays)
+
+
+def fused(queries, keys, values, out_weight, mixed_grad, lengths, dilation, groups, chunks=4):
+    rows, cols = queries.shape
+    width = HEAD_WIDTH
+    heads = cols // GROUP // width
+    feats = mixed_grad.shape[1]
+    step = feats // chunks
+    block, halo, tokens = 2 * rows, 2 * rows, GROUP * rows
+    window = block + 2 * halo
+    hbm = pl.BlockSpec(memory_space=pltpu.HBM)
+    vmem = pl.BlockSpec(memory_space=pl.ANY)
+    dma = pltpu.SemaphoreType.DMA
+    V = pltpu.VMEM
+    one = jax.ShapeDtypeStruct((rows, cols), BF16)
+    big = [
+        pltpu.with_memory_space_constraint(a, pltpu.HBM)
+        for a in (lengths, dilation, queries, keys, values, out_weight, mixed_grad)
+    ]
+    outs = pl.pallas_call(
+        functools.partial(fused_kernel, groups),
+        in_specs=[hbm] * 7,
+        out_specs=[vmem] * 4,
+        out_shape=[jax.ShapeDtypeStruct((rows, feats), BF16), one, one, one],
+        scratch_shapes=[
+            V((cols, feats), BF16), V((cols, feats), BF16),
+            V((rows, feats), BF16), V((chunks, rows, step), BF16),
+            V((heads, 2, tokens + 2 * halo, width), BF16),
+            V((heads, tokens, width), BF16), V((heads, tokens, width), BF16),
+            V((rows, cols), F32), V((rows, cols), BF16),
+            V((heads, tokens, width), BF16), V((rows, cols), BF16),
+            V((chunks, rows, step), BF16), V((chunks, rows, step), BF16), V((chunks, rows, step), F32),
+            V((2, heads, window, block), BF16), V((heads, window, block), jnp.int32),
+            V((2, heads, 8, block), jnp.int32), V((2, heads, 2, 2 * block, width), F32),
+            V((2, heads, window, block), BF16),
+            V((2, heads, 2, halo, width), BF16), V((2, heads, 2, halo, width), BF16),
+            V((heads, tokens, width), BF16), V((heads, 2, tokens, width), BF16),
+            V((chunks, rows, step), BF16), pltpu.SMEM(lengths.shape, jnp.int32), pltpu.SMEM(dilation.shape, jnp.int32),
+            dma((2,)), dma((2,)), dma, dma, dma((chunks,)), dma((GROUP - 1, heads)), dma((heads,)),
+            dma((2, heads)), dma((heads,)), dma, dma((chunks,)), dma((2, heads, 2)), dma((3,)), dma,
+            dma, dma, dma,
+        ],
+        compiler_params=pltpu.CompilerParams(
+            collective_id=0, has_side_effects=True, vmem_limit_bytes=32 * 1024 * 1024
+        ),
+    )(*big)
+    return tuple(store(outs))
 
 
 def attend_kernel(
@@ -110,6 +642,11 @@
     sides = lax.axis_size("head")
     total = rows * count
     assert 2 * rows >= HALF * MAXD and count % 2 == 0
+    if sides == 2 and count % GROUP == 0 and local_heads % GROUP == 0 and width == HEAD_WIDTH:
+        if 2 * rows == HALF * MAXD and mixed_grad.shape[1] % 512 == 0:
+            return fused(
+                queries, keys, values, out_weight, mixed_grad, lengths, dilation, count // GROUP
+            )
     index = lax.axis_index("ctx").astype(jnp.int32).reshape(1)
 
     inward = [

time: 82.5 us -> 36.1 us (0.44)
  waiting for transfers between devices: 29.5 us -> 0 us
  Pallas kernels: 10 us -> 35.3 us
  starting transfers between devices: 23 us -> 0 us
  matrix products: 11.8 us -> 0 us
  other arithmetic: 5.68 us -> 0 us
  local copies, waits for them, and re-layouts: 0.83 us -> 0 us
    ppermute x10 -> x0, waiting for transfers between devices: 29.5 us -> none  [the longest x8 15.8 us: move(): return lax.ppermute(x, 'ctx', pairs)]
    pallas_call x1 -> x2, Pallas kernels: 10 us -> 35.3 us  [the longest x1 34.2 us: fused(): pl.pallas_call(functools.partial(fused_kernel, groups), in_specs=[hbm] *...]
    ppermute x10 -> x0, starting transfers between devices: 23 us -> none  [the longest x8 19.4 us: move(): return lax.ppermute(x, 'ctx', pairs)]
    dot_general x2 -> x0, matrix products: 11.8 us -> none  [the longest x1 6.97 us: per_device(): lax.dot_general(grad_full, out_weight, (((1,), (1,)), ((), ())), preferre...]
    convert_element_type x3 -> x0, other arithmetic: 2.34 us -> none  [the longest x1 1.24 us: per_device(): a_sum = (a_t.astype(f32) + pa_back.astype(f32)).astype(jnp.bfloat16)]
    add x1 -> x0, other arithmetic: 1.14 us -> none  [per_device(): sum((term[i].astype(f32) for term in terms)).astype(jnp.bfloat16)]
    select_n x1 -> x0, other arithmetic: 1.11 us -> none  [per_device(): jnp.where(left, mixed_grad, other)]
    another operation x1 -> x0, other arithmetic: 1.08 us -> none  [per_device(): own = jnp.stack([keys[:, cut[g]], values[:, cut[g]]])]
  transfers between devices with their start and end apart: 10 -> 0, of which waited for: 5 -> 0; matrix products, arithmetic and copies ran while one was open for 12% -> 0% of each run, Pallas kernels for 0% -> 0%
where the time goes in v1:
time: 36.1 us; the launch traced here: 35.9 us
  Pallas kernels  35.3 us (98%)
  between operations  0.64 us (2%)
    pallas_call x1, Pallas kernels, fused(): pl.pallas_call(functools.partial(fused_kernel, groups), in_specs=[hbm] *...  34.2 us
    pallas_call x1, Pallas kernels, store(): pl.pallas_call(store_kernel, in_specs=[pl.BlockSpec(memory_space=pltpu.VM...  1.09 us

profile of v1, /device:TPU:0, one launch (start us, length us, event | category | flops | bytes accessed | tf_op | source)
XLA Modules:
  0.0 35.9 jit_solution(4958329389691083141)
XLA Ops:
  0.6 34.2 %shard_map.102 = (bf16[128,2048]{1,0:T(8,128)(2,1)S(1)}, bf16[128,1024]{1,0:T(8,128)(2,1)S(1)}, bf16[128,1024]{1,0:T(8,128)(2,1)S(1)}, bf16[128,1024]{1,0:T(8,128)(2,1)S(1)}) custom-call(s32[16]{0:T(128)} %length_hbm.1, s32[8]{0:T(128)} %dilation_hbm.1, bf16[128,1024]{1,0:T(8,128)(2,1)} %q_ref.1, bf16[128,1024]{1,0:T(8,128)(2,1)} %k_ref.1, ...), custom_call_target="tpu_custom_call" | custom-call | tf_op jit(solution)/shard_map/pallas_call | solution.py:517
  34.9 1.1 %shard_map.103 = (bf16[128,2048]{1,0:T(8,128)(2,1)}, bf16[128,1024]{1,0:T(8,128)(2,1)}, bf16[128,1024]{1,0:T(8,128)(2,1)}, bf16[128,1024]{1,0:T(8,128)(2,1)}) custom-call(bf16[128,2048]{1,0:T(8,128)(2,1)S(1)} %get-tuple-element.8.refs_0_, bf16[128,1024]{1,0:T(8,128)(2,1)S(1)} %get-tuple-element.9.refs_1_, bf16[128,1024]{1,0:T(8,128)(2,1)S(1)} %get-tuple-element.10.refs_2_, ...), custom_call_target="tpu_custom_call" | custom-call | tf_op jit(solution)/shard_map/pallas_call | solution.py:490

commit v2 on v1

--- a/solution.py
+++ b/solution.py
@@ -16,6 +16,7 @@
 NT = (((1,), (1,)), ((), ()))
 TN = (((0,), (0,)), ((), ()))
 F32 = jnp.float32
+LOG2E = 1.4426950408889634
 BF16 = jnp.bfloat16
 MESH_ID = pl.DeviceIdType.MESH
 
@@ -24,7 +25,7 @@
     groups, length_hbm, dilation_hbm, q_ref, k_ref, v_ref, w_ref, mg_ref,
     mixed_ref, gq_ref, gk_ref, gv_ref,
     w_own, w_oth, mg_own, mg_oth, kv, qs, gos, go_acc, go_bf, att_my, att_in,
-    part_send, part_recv, part_own, probs, spaced, bounds, terms,
+    part_send, part_recv, part_own, probs, spaced, bias, terms,
     slopes, halo_send, halo_recv, dq, dkv, mixed_out, length_ref, dilation_ref,
     int_sem, w_sem, mg_sem, own_sem, x_recv, kv_recv, q_recv, halo_kv, go_recv, att_recv,
     p_recv, h_recv, out_recv, mixed_sem, sent, sent_fwd, sent_bwd,
@@ -109,7 +110,7 @@
 
     def own(t, h):
         source = (k_ref, v_ref, q_ref)[t].at[:, lanes(r, h)]
-        return pltpu.make_async_copy(source, in_place(t, h), own_sem if t < 2 else q_recv.at[h])
+        return pltpu.make_async_copy(source, in_place(t, h), own_sem if t < 2 else q_recv.at[0, h])
 
     mg_copy = pltpu.make_async_copy(mg_ref, mg_own, mg_sem)
     for h in range(heads):
@@ -131,7 +132,7 @@
 
     def in_copy(t, o, h):
         source = (k_ref, v_ref, q_ref)[t].at[:, lanes(peers[o], h)]
-        recv = kv_recv.at[o - 1, h] if t < 2 else q_recv.at[h]
+        recv = kv_recv.at[o - 1, h] if t < 2 else q_recv.at[o // 2, h]
         return remote(source, in_place(t, h), sent, recv, peer_id(o))
 
     with scope("send"):
@@ -185,7 +186,25 @@
 
     for copy in integers:
         copy.wait()
-    with scope("masks"):
+    def masks(i):
+        first = base * rows + (1 - y if i == 0 else y) * block
+        qpos = first + lax.broadcasted_iota(jnp.int32, (1, block), 1)
+        start = jnp.zeros((1, block), jnp.int32)
+        stop = jnp.full((1, block), 1 << 24, jnp.int32)
+        end = jnp.int32(0)
+        for n in range(length_ref.shape[0]):
+            end = end + length_ref[n]
+            past = qpos >= end
+            start = jnp.where(past, jnp.maximum(start, end), start)
+            stop = jnp.where(past, stop, jnp.minimum(stop, end))
+        for h in range(heads):
+            reach = jnp.full((1, block), HALF * dilation_ref[r * heads + h], jnp.int32)
+            lo = jnp.maximum(start - qpos, -reach)
+            hi = jnp.minimum(stop - 1 - qpos, reach)
+            rel = spaced[h]
+            bias[i, h] = jnp.where((rel >= lo) & (rel <= hi), 0.0, NEG)
+
+    with scope("spaced"):
         rel = lax.broadcasted_iota(jnp.int32, (window, block), 0) - halo
         rel = rel - lax.broadcasted_iota(jnp.int32, (window, block), 1)
         relf = rel.astype(F32)
@@ -193,22 +212,8 @@
             spacing = jnp.full((1, block), dilation_ref[r * heads + h], jnp.int32)
             inv = 1.0 / spacing.astype(F32)
             steps = relf * inv
-            whole = jnp.floor(steps + 0.5)
-            spaced[h] = jnp.where(jnp.abs(steps - whole) < 0.01, rel, 1 << 24)
-        for b in range(2):
-            qpos = base * rows + b * block + lax.broadcasted_iota(jnp.int32, (1, block), 1)
-            start = jnp.zeros((1, block), jnp.int32)
-            stop = jnp.full((1, block), 1 << 24, jnp.int32)
-            end = jnp.int32(0)
-            for n in range(length_ref.shape[0]):
-                end = end + length_ref[n]
-                past = qpos >= end
-                start = jnp.where(past, jnp.maximum(start, end), start)
-                stop = jnp.where(past, stop, jnp.minimum(stop, end))
-            for h in range(heads):
-                reach = jnp.full((1, block), HALF * dilation_ref[r * heads + h], jnp.int32)
-                bounds[b, h, 0:1, :] = jnp.maximum(start - qpos, -reach)
-                bounds[b, h, 1:2, :] = jnp.minimum(stop - 1 - qpos, reach)
+            near = jnp.floor(steps + 0.5)
+            spaced[h] = jnp.where(jnp.abs(steps - near) < 0.01, rel, 1 << 24)
 
     def go_step(mg, weight, first):
         term = lax.dot_general(mg, weight, NT, preferred_element_type=F32)
@@ -231,6 +236,9 @@
         with scope("go_far"):
             go_step(mg_oth[n], w_oth[:, part(n)], False)
 
+    with scope("masks"):
+        for i in range(2):
+            masks(i)
     with scope("wait_kv"):
         for h in range(heads):
             pass_on(1, h)
@@ -241,24 +249,26 @@
     def at_rows(i):
         return pl.multiple_of((1 - y) * block if i == 0 else y * block, block)
 
+    def whole(i):
+        return pl.ds(at_rows(i), block), pl.ds(0, block)
+
+    def far_part(o):
+        return slab(peers[o]), slab(peers[o] - 2 * (1 - y))
+
     def forward(i, h):
         row0 = at_rows(i)
-        b = 1 - y if i == 0 else y
         k = kv[h, 0, pl.ds(row0, window), :]
         v = kv[h, 1, pl.ds(row0, window), :]
-        q = qs[h, pl.ds(row0, block), :]
-        s = lax.dot_general(k, q, NT, preferred_element_type=F32)
-        rel = spaced[h]
-        lo = bounds[b, h, 0:1, :]
-        hi = bounds[b, h, 1:2, :]
-        s = jnp.where((rel >= lo) & (rel <= hi), s, NEG)
+        q_rows = pl.ds(row0, block)
+        s = lax.dot_general(k, qs[h, q_rows, :], NT, preferred_element_type=F32)
+        s = s + bias[i, h]
         top = jnp.max(s, axis=0, keepdims=True)
-        e = jnp.exp((s - top) * factor)
+        e = jnp.exp2((s - top) * (factor * LOG2E))
         w = e * (1.0 / jnp.sum(e, axis=0, keepdims=True))
         p = w.astype(BF16)
         probs[i, h] = p
         att = lax.dot_general(p, v, TN, preferred_element_type=F32)
-        att_my[h, pl.ds(row0, block), :] = att.astype(BF16)
+        att_my[h, q_rows, :] = att.astype(BF16)
 
     def att_copy(o, h):
         return remote(
@@ -272,48 +282,62 @@
         )
 
     def near_block(h):
-        with scope("wait_q"):
-            arrived(qs.at[h], q_recv.at[h])
-
         @pl.when(has_bwd)
         def _():
             with scope("wait_near"):
                 arrived(kv.at[h, :, pl.ds(near_row, halo), :], halo_kv.at[0, h])
 
+        with scope("wait_q"):
+            arrived(qs.at[h, pl.ds(at_rows(0), block), :], q_recv.at[1, h])
         with scope("forward"):
             forward(0, h)
         for o in (2, 3):
             att_copy(o, h).start()
 
-    def far_block(h):
+    def far_blocks():
         @pl.when(has_fwd)
         def _():
             with scope("wait_far"):
-                arrived(kv.at[h, :, pl.ds(far_row, halo), :], halo_kv.at[1, h])
-
+                for h in range(heads):
+                    arrived(kv.at[h, :, pl.ds(far_row, halo), :], halo_kv.at[1, h])
+
+        with scope("wait_q"):
+            for h in range(heads):
+                arrived(qs.at[h, pl.ds(at_rows(1), block), :], q_recv.at[0, h])
         with scope("forward"):
-            forward(1, h)
-        att_copy(1, h).start()
-        att_local(h).start()
+            for h in range(heads):
+                forward(1, h)
+        for h in range(heads):
+            att_copy(1, h).start()
+            att_local(h).start()
 
     go_far(0)
     for h in range(heads):
         near_block(h)
-        far_block(h)
-    for n in range(1, chunks):
+    go_far(1)
+    far_blocks()
+    for n in range(2, chunks - 1):
         go_far(n)
 
     def go_copy(o, h):
         return remote(
             go_bf.at[:, lanes(peers[o], h)], gos.at[h, slab(r), :],
-            sent, go_recv.at[h], peer_id(o),
+            sent, go_recv.at[o // 2 * (o - 1), h], peer_id(o),
         )
 
     def go_local(h):
-        return pltpu.make_async_copy(go_bf.at[:, lanes(r, h)], gos.at[h, slab(r), :], go_recv.at[h])
-
-    go_bf[...] = go_acc[...].astype(BF16)
+        return pltpu.make_async_copy(go_bf.at[:, lanes(r, h)], gos.at[h, slab(r), :], go_recv.at[0, h])
+
+    with scope("wait_x"):
+        x_copy(chunks - 1).wait_recv()
     for h in range(heads):
+        with scope("go_last"):
+            for i in range(GROUP):
+                at = slice((i * heads + h) * width, (i * heads + h + 1) * width)
+                term = lax.dot_general(
+                    mg_oth[chunks - 1], w_oth[at, part(chunks - 1)], NT, preferred_element_type=F32
+                )
+                go_bf[:, at] = (go_acc[:, at] + term).astype(BF16)
         for o in (2, 3, 1):
             go_copy(o, h).start()
         go_local(h).start()
@@ -324,15 +348,13 @@
     def p_copy(n):
         return remote(part_send.at[n], part_recv.at[n], sent, p_recv.at[n], x_id)
 
-    for n in range(chunks):
+    def project(n):
         with scope("proj_far"):
             term = jnp.dot(att_in[...], w_oth[:, part(n)], preferred_element_type=F32)
             part_send[n] = term.astype(BF16)
         p_copy(n).start()
 
-    with scope("proj_own"):
-        for n in range(chunks):
-            part_own[n] = jnp.dot(att_in[...], w_own[:, part(n)], preferred_element_type=F32)
+    project(0)
 
     def edge_rows(i):
         return pl.ds(pl.multiple_of(2 * at_rows(i), block), block)
@@ -342,23 +364,22 @@
         dv = jnp.dot(probs[i, h, edge_rows(i), :], go, preferred_element_type=F32)
         halo_send[i, h, 1] = dv.astype(BF16)
 
+    def slope_terms(i, h, q_rows, cols):
+        v = kv[h, 1, pl.ds(at_rows(i), window), :]
+        gp = lax.dot_general(v, gos[h, q_rows, :], NT, preferred_element_type=F32)
+        w = probs[i, h, :, cols].astype(F32)
+        delta = jnp.sum(w * gp, axis=0, keepdims=True)
+        slopes[i, h, :, cols] = (w * (gp - delta)).astype(BF16)
+
     def edge_keys(i, h):
-        row0 = at_rows(i)
-        v = kv[h, 1, pl.ds(row0, window), :]
-        q = qs[h, pl.ds(row0, block), :]
-        go = gos[h, pl.ds(row0, block), :]
-        gp = lax.dot_general(v, go, NT, preferred_element_type=F32)
-        w = probs[i, h].astype(F32)
-        delta = jnp.sum(w * gp, axis=0, keepdims=True)
-        slopes[i, h] = (w * (gp - delta)).astype(BF16)
+        q = qs[h, pl.ds(at_rows(i), block), :]
         dk = jnp.dot(slopes[i, h, edge_rows(i), :], q, preferred_element_type=F32) * factor
         halo_send[i, h, 0] = dk.astype(BF16)
 
-    def query_terms(i, h):
-        row0 = at_rows(i)
-        k = kv[h, 0, pl.ds(row0, window), :]
-        gq = lax.dot_general(slopes[i, h], k, TN, preferred_element_type=F32) * factor
-        dq[h, pl.ds(row0, block), :] = gq.astype(BF16)
+    def query_terms(i, h, q_rows, cols):
+        k = kv[h, 0, pl.ds(at_rows(i), window), :]
+        gq = lax.dot_general(slopes[i, h, :, cols], k, TN, preferred_element_type=F32) * factor
+        dq[h, q_rows, :] = gq.astype(BF16)
 
     def inner_terms(i, h):
         row0 = at_rows(i)
@@ -389,27 +410,24 @@
             source.at[slab(r), :], results[t].at[:, lanes(r, h)], out_recv.at[t]
         )
 
-    def sums(t, h):
-        @pl.when(has_fwd)
+    def sums(i, t, h):
+        @pl.when(has_fwd if i == 0 else has_bwd)
         def _():
-            with scope("wait_h0"):
-                arrived(halo_recv.at[0, h, t], h_recv.at[0, h, t])
-
-        @pl.when(has_bwd)
-        def _():
-            with scope("wait_h1"):
-                arrived(halo_recv.at[1, h, t], h_recv.at[1, h, t])
+            with scope("wait_far_sum" if i else "wait_near_sum"):
+                arrived(halo_recv.at[i, h, t], h_recv.at[i, h, t])
 
         with scope("sums"):
-            for i in range(2):
-                half = pl.multiple_of(y * block if i == 0 else (1 - y) * block, block)
-                out = pl.ds(half, block)
-                total = terms[0, h, t, out, :] + terms[1, h, t, out, :]
-                total = total + halo_recv[i, h, t].astype(F32)
-                dkv[h, t, out, :] = total.astype(BF16)
-        for o in (2, 3, 1):
-            out_copy(1 + t, o, h).start()
-        out_local(1 + t, h).start()
+            half = pl.multiple_of(y * block if i == 0 else (1 - y) * block, block)
+            out = pl.ds(half, block)
+            total = terms[0, h, t, out, :] + terms[1, h, t, out, :]
+            total = total + halo_recv[i, h, t].astype(F32)
+            dkv[h, t, out, :] = total.astype(BF16)
+        if i == 0:
+            out_copy(1 + t, 1, h).start()
+            out_local(1 + t, h).start()
+        else:
+            out_copy(1 + t, 2, h).start()
+            out_copy(1 + t, 3, h).start()
 
     def send_edge(t, i, h):
         with scope("edge"):
@@ -419,28 +437,56 @@
         def _():
             h_copy(i, h, t).start()
 
+    def own_queries(h):
+        with scope("wait_go"):
+            arrived(gos.at[h, pl.ds(at_rows(1), block), :], go_recv.at[0, h])
+        send_edge(1, 1, h)
+        with scope("slopes"):
+            slope_terms(1, h, *whole(1))
+        send_edge(0, 1, h)
+
+    def far_queries(h):
+        for group in ((2,), (3,)) if h == 0 else ((2, 3),):
+            with scope("wait_go"):
+                for o in group:
+                    arrived(gos.at[h, slab(peers[o]), :], go_recv.at[o - 1, h])
+            with scope("slopes"):
+                at = whole(0) if len(group) == 2 else far_part(group[0])
+                slope_terms(0, h, *at)
+                query_terms(0, h, *at)
+            for o in group:
+                out_copy(0, o, h).start()
+
+    own_queries(0)
+    project(1)
     for h in range(heads):
-        with scope("wait_go"):
-            arrived(gos.at[h], go_recv.at[h])
-        for i in range(2):
-            send_edge(1, i, h)
-        for i in range(2):
-            send_edge(0, i, h)
-            if h > 0:
-                sums(1 - i, h - 1)
-            with scope("query"):
-                query_terms(i, h)
-            if i == 0:
-                out_copy(0, 2, h).start()
-                out_copy(0, 3, h).start()
-            else:
-                out_copy(0, 1, h).start()
-                out_local(0, h).start()
+        far_queries(h)
+        send_edge(0, 0, h)
+        send_edge(1, 0, h)
+        if h > 0:
+            sums(1, 0, h - 1)
         with scope("inner"):
             for i in range(2):
                 inner_terms(i, h)
-    for t in (1, 0):
-        sums(t, heads - 1)
+        if h + 1 < heads:
+            own_queries(h + 1)
+        sums(1, 1, h)
+        if h + 2 < chunks:
+            project(h + 2)
+    for n in range(heads + 2, chunks):
+        project(n)
+    sums(1, 0, heads - 1)
+    for h in range(heads):
+        with scope("query"):
+            query_terms(1, h, *whole(1))
+        out_copy(0, 1, h).start()
+        out_local(0, h).start()
+    for h in range(heads):
+        for t in (1, 0):
+            sums(0, t, h)
+    with scope("proj_own"):
+        for n in range(chunks):
+            part_own[n] = jnp.dot(att_in[...], w_own[:, part(n)], preferred_element_type=F32)
 
     def mixed_copy(n):
         return pltpu.make_async_copy(
@@ -528,13 +574,13 @@
             V((heads, tokens, width), BF16), V((rows, cols), BF16),
             V((chunks, rows, step), BF16), V((chunks, rows, step), BF16), V((chunks, rows, step), F32),
             V((2, heads, window, block), BF16), V((heads, window, block), jnp.int32),
-            V((2, heads, 8, block), jnp.int32), V((2, heads, 2, 2 * block, width), F32),
+            V((2, heads, window, block), F32), V((2, heads, 2, 2 * block, width), F32),
             V((2, heads, window, block), BF16),
             V((2, heads, 2, halo, width), BF16), V((2, heads, 2, halo, width), BF16),
             V((heads, tokens, width), BF16), V((heads, 2, tokens, width), BF16),
             V((chunks, rows, step), BF16), pltpu.SMEM(lengths.shape, jnp.int32), pltpu.SMEM(dilation.shape, jnp.int32),
-            dma((2,)), dma((2,)), dma, dma, dma((chunks,)), dma((GROUP - 1, heads)), dma((heads,)),
-            dma((2, heads)), dma((heads,)), dma, dma((chunks,)), dma((2, heads, 2)), dma((3,)), dma,
+            dma((2,)), dma((2,)), dma, dma, dma((chunks,)), dma((GROUP - 1, heads)), dma((2, heads)),
+            dma((2, heads)), dma((3, heads)), dma, dma((chunks,)), dma((2, heads, 2)), dma((3,)), dma,
             dma, dma, dma,
         ],
         compiler_params=pltpu.CompilerParams(

time: 36.1 us -> 34.7 us (0.961)
  Pallas kernels: 35.3 us -> 33.9 us
    pallas_call x1, Pallas kernels: 34.2 us -> 32.8 us  [fused(): pl.pallas_call(functools.partial(fused_kernel, groups), in_specs=[hbm] *...]
where the time goes in v2:
time: 34.7 us; the launch traced here: 34.6 us
  Pallas kernels  33.9 us (98%)
  between operations  0.64 us (2%)
    pallas_call x1, Pallas kernels, fused(): pl.pallas_call(functools.partial(fused_kernel, groups), in_specs=[hbm] *...  32.8 us
    pallas_call x1, Pallas kernels, store(): pl.pallas_call(store_kernel, in_specs=[pl.BlockSpec(memory_space=pltpu.VM...  1.09 us

profile of v2, /device:TPU:0, one launch (start us, length us, event | category | flops | bytes accessed | tf_op | source)
XLA Modules:
  0.0 34.6 jit_solution(5872736131879691394)
XLA Ops:
  0.6 32.8 %shard_map.102 = (bf16[128,2048]{1,0:T(8,128)(2,1)S(1)}, bf16[128,1024]{1,0:T(8,128)(2,1)S(1)}, bf16[128,1024]{1,0:T(8,128)(2,1)S(1)}, bf16[128,1024]{1,0:T(8,128)(2,1)S(1)}) custom-call(s32[16]{0:T(128)} %length_hbm.1, s32[8]{0:T(128)} %dilation_hbm.1, bf16[128,1024]{1,0:T(8,128)(2,1)} %q_ref.1, bf16[128,1024]{1,0:T(8,128)(2,1)} %k_ref.1, ...), custom_call_target="tpu_custom_call" | custom-call | tf_op jit(solution)/shard_map/pallas_call | solution.py:563
  33.5 1.1 %shard_map.103 = (bf16[128,2048]{1,0:T(8,128)(2,1)}, bf16[128,1024]{1,0:T(8,128)(2,1)}, bf16[128,1024]{1,0:T(8,128)(2,1)}, bf16[128,1024]{1,0:T(8,128)(2,1)}) custom-call(bf16[128,2048]{1,0:T(8,128)(2,1)S(1)} %get-tuple-element.8.refs_0_, bf16[128,1024]{1,0:T(8,128)(2,1)S(1)} %get-tuple-element.9.refs_1_, bf16[128,1024]{1,0:T(8,128)(2,1)S(1)} %get-tuple-element.10.refs_2_, ...), custom_call_target="tpu_custom_call" | custom-call | tf_op jit(solution)/shard_map/pallas_call | solution.py:536

commit v3 on v2

--- a/solution.py
+++ b/solution.py
@@ -132,7 +132,7 @@
 
     def in_copy(t, o, h):
         source = (k_ref, v_ref, q_ref)[t].at[:, lanes(peers[o], h)]
-        recv = kv_recv.at[o - 1, h] if t < 2 else q_recv.at[o // 2, h]
+        recv = kv_recv.at[o - 1, h] if t < 2 else q_recv.at[o // 2 * (o - 1), h]
         return remote(source, in_place(t, h), sent, recv, peer_id(o))
 
     with scope("send"):
@@ -255,18 +255,17 @@
     def far_part(o):
         return slab(peers[o]), slab(peers[o] - 2 * (1 - y))
 
-    def forward(i, h):
+    def forward(i, h, q_rows, cols):
         row0 = at_rows(i)
         k = kv[h, 0, pl.ds(row0, window), :]
         v = kv[h, 1, pl.ds(row0, window), :]
-        q_rows = pl.ds(row0, block)
         s = lax.dot_general(k, qs[h, q_rows, :], NT, preferred_element_type=F32)
-        s = s + bias[i, h]
+        s = s + bias[i, h, :, cols]
         top = jnp.max(s, axis=0, keepdims=True)
         e = jnp.exp2((s - top) * (factor * LOG2E))
         w = e * (1.0 / jnp.sum(e, axis=0, keepdims=True))
         p = w.astype(BF16)
-        probs[i, h] = p
+        probs[i, h, :, cols] = p
         att = lax.dot_general(p, v, TN, preferred_element_type=F32)
         att_my[h, q_rows, :] = att.astype(BF16)
 
@@ -287,12 +286,14 @@
             with scope("wait_near"):
                 arrived(kv.at[h, :, pl.ds(near_row, halo), :], halo_kv.at[0, h])
 
-        with scope("wait_q"):
-            arrived(qs.at[h, pl.ds(at_rows(0), block), :], q_recv.at[1, h])
-        with scope("forward"):
-            forward(0, h)
-        for o in (2, 3):
-            att_copy(o, h).start()
+        for group in ((2,), (3,)) if h == 0 else ((2, 3),):
+            with scope("wait_q"):
+                for o in group:
+                    arrived(qs.at[h, slab(peers[o]), :], q_recv.at[o - 1, h])
+            with scope("forward"):
+                forward(0, h, *(whole(0) if len(group) == 2 else far_part(group[0])))
+            for o in group:
+                att_copy(o, h).start()
 
     def far_blocks():
         @pl.when(has_fwd)
@@ -306,7 +307,7 @@
                 arrived(qs.at[h, pl.ds(at_rows(1), block), :], q_recv.at[0, h])
         with scope("forward"):
             for h in range(heads):
-                forward(1, h)
+                forward(1, h, *whole(1))
         for h in range(heads):
             att_copy(1, h).start()
             att_local(h).start()
@@ -345,16 +346,23 @@
     with scope("wait_att"):
         arrived(att_in, att_recv)
 
-    def p_copy(n):
-        return remote(part_send.at[n], part_recv.at[n], sent, p_recv.at[n], x_id)
-
-    def project(n):
-        with scope("proj_far"):
-            term = jnp.dot(att_in[...], w_oth[:, part(n)], preferred_element_type=F32)
-            part_send[n] = term.astype(BF16)
-        p_copy(n).start()
-
-    project(0)
+    def p_copy(n, cols):
+        return remote(
+            part_send.at[n, :, cols], part_recv.at[n, :, cols], sent, p_recv.at[n], x_id
+        )
+
+    def project(n, pieces=1):
+        size = step // pieces
+        for i in range(pieces):
+            with scope("proj_far"):
+                at = n * step + i * size
+                term = jnp.dot(
+                    att_in[...], w_oth[:, at : at + size], preferred_element_type=F32
+                )
+                part_send[n, :, i * size : (i + 1) * size] = term.astype(BF16)
+            p_copy(n, pl.ds(i * size, size)).start()
+
+    project(0, 4)
 
     def edge_rows(i):
         return pl.ds(pl.multiple_of(2 * at_rows(i), block), block)
@@ -495,7 +503,7 @@
 
     for n in range(chunks):
         with scope("wait_part"):
-            p_copy(n).wait_recv()
+            arrived(part_recv.at[n], p_recv.at[n])
         with scope("mixed"):
             total = part_own[n] + part_recv[n].astype(F32)
             mixed_out[n] = total.astype(BF16)
@@ -579,7 +587,7 @@
             V((2, heads, 2, halo, width), BF16), V((2, heads, 2, halo, width), BF16),
             V((heads, tokens, width), BF16), V((heads, 2, tokens, width), BF16),
             V((chunks, rows, step), BF16), pltpu.SMEM(lengths.shape, jnp.int32), pltpu.SMEM(dilation.shape, jnp.int32),
-            dma((2,)), dma((2,)), dma, dma, dma((chunks,)), dma((GROUP - 1, heads)), dma((2, heads)),
+            dma((2,)), dma((2,)), dma, dma, dma((chunks,)), dma((GROUP - 1, heads)), dma((3, heads)),
             dma((2, heads)), dma((3, heads)), dma, dma((chunks,)), dma((2, heads, 2)), dma((3,)), dma,
             dma, dma, dma,
         ],

time: 34.7 us -> 34.3 us (0.988)
  Pallas kernels: 33.9 us -> 33.5 us
    pallas_call x1, Pallas kernels: 32.8 us -> 32.5 us  [fused(): pl.pallas_call(functools.partial(fused_kernel, groups), in_specs=[hbm] *...]
where the time goes in v3:
time: 34.3 us; the launch traced here: 34.2 us
  Pallas kernels  33.5 us (98%)
  between operations  0.64 us (2%)
    pallas_call x1, Pallas kernels, fused(): pl.pallas_call(functools.partial(fused_kernel, groups), in_specs=[hbm] *...  32.5 us
    pallas_call x1, Pallas kernels, store(): pl.pallas_call(store_kernel, in_specs=[pl.BlockSpec(memory_space=pltpu.VM...  1.09 us

profile of v3, /device:TPU:0, one launch (start us, length us, event | category | flops | bytes accessed | tf_op | source)
XLA Modules:
  0.0 34.2 jit_solution(7768050250958656230)
XLA Ops:
  0.6 32.5 %shard_map.102 = (bf16[128,2048]{1,0:T(8,128)(2,1)S(1)}, bf16[128,1024]{1,0:T(8,128)(2,1)S(1)}, bf16[128,1024]{1,0:T(8,128)(2,1)S(1)}, bf16[128,1024]{1,0:T(8,128)(2,1)S(1)}) custom-call(s32[16]{0:T(128)} %length_hbm.1, s32[8]{0:T(128)} %dilation_hbm.1, bf16[128,1024]{1,0:T(8,128)(2,1)} %q_ref.1, bf16[128,1024]{1,0:T(8,128)(2,1)} %k_ref.1, ...), custom_call_target="tpu_custom_call" | custom-call | tf_op jit(solution)/shard_map/pallas_call | solution.py:571
  33.1 1.1 %shard_map.103 = (bf16[128,2048]{1,0:T(8,128)(2,1)}, bf16[128,1024]{1,0:T(8,128)(2,1)}, bf16[128,1024]{1,0:T(8,128)(2,1)}, bf16[128,1024]{1,0:T(8,128)(2,1)}) custom-call(bf16[128,2048]{1,0:T(8,128)(2,1)S(1)} %get-tuple-element.8.refs_0_, bf16[128,1024]{1,0:T(8,128)(2,1)S(1)} %get-tuple-element.9.refs_1_, bf16[128,1024]{1,0:T(8,128)(2,1)S(1)} %get-tuple-element.10.refs_2_, ...), custom_call_target="tpu_custom_call" | custom-call | tf_op jit(solution)/shard_map/pallas_call | solution.py:544

commit v4 on v3

--- a/solution.py
+++ b/solution.py
@@ -489,12 +489,12 @@
             query_terms(1, h, *whole(1))
         out_copy(0, 1, h).start()
         out_local(0, h).start()
+    with scope("proj_own"):
+        for n in range(chunks):
+            part_own[n] = jnp.dot(att_in[...], w_own[:, part(n)], preferred_element_type=F32)
     for h in range(heads):
         for t in (1, 0):
             sums(0, t, h)
-    with scope("proj_own"):
-        for n in range(chunks):
-            part_own[n] = jnp.dot(att_in[...], w_own[:, part(n)], preferred_element_type=F32)
 
     def mixed_copy(n):
         return pltpu.make_async_copy(

time: 34.3 us -> 34.3 us (level)
  no operation moved by 1% of the time
where the time goes in v4:
time: 34.3 us; the launch traced here: 34.2 us
  Pallas kernels  33.5 us (98%)
  between operations  0.64 us (2%)
    pallas_call x1, Pallas kernels, fused(): pl.pallas_call(functools.partial(fused_kernel, groups), in_specs=[hbm] *...  32.5 us
    pallas_call x1, Pallas kernels, store(): pl.pallas_call(store_kernel, in_specs=[pl.BlockSpec(memory_space=pltpu.VM...  1.09 us

profile of v4, /device:TPU:0, one launch (start us, length us, event | category | flops | bytes accessed | tf_op | source)
XLA Modules:
  0.0 34.2 jit_solution(8621378456081787576)
XLA Ops:
  0.6 32.5 %shard_map.102 = (bf16[128,2048]{1,0:T(8,128)(2,1)S(1)}, bf16[128,1024]{1,0:T(8,128)(2,1)S(1)}, bf16[128,1024]{1,0:T(8,128)(2,1)S(1)}, bf16[128,1024]{1,0:T(8,128)(2,1)S(1)}) custom-call(s32[16]{0:T(128)} %length_hbm.1, s32[8]{0:T(128)} %dilation_hbm.1, bf16[128,1024]{1,0:T(8,128)(2,1)} %q_ref.1, bf16[128,1024]{1,0:T(8,128)(2,1)} %k_ref.1, ...), custom_call_target="tpu_custom_call" | custom-call | tf_op jit(solution)/shard_map/pallas_call | solution.py:571
  33.1 1.1 %shard_map.103 = (bf16[128,2048]{1,0:T(8,128)(2,1)}, bf16[128,1024]{1,0:T(8,128)(2,1)}, bf16[128,1024]{1,0:T(8,128)(2,1)}, bf16[128,1024]{1,0:T(8,128)(2,1)}) custom-call(bf16[128,2048]{1,0:T(8,128)(2,1)S(1)} %get-tuple-element.8.refs_0_, bf16[128,1024]{1,0:T(8,128)(2,1)S(1)} %get-tuple-element.9.refs_1_, bf16[128,1024]{1,0:T(8,128)(2,1)S(1)} %get-tuple-element.10.refs_2_, ...), custom_call_target="tpu_custom_call" | custom-call | tf_op jit(solution)/shard_map/pallas_call | solution.py:544
